TPU v7x, 32 devices: a whole 2x2x4 slice. The times are simulated.
32 devices in a mesh: row: 4 (over z), col: 4 (over y, core), rep: 2 (over x).
Axes of the slice: x: 2, y: 2, z: 4, core: 2. Of those that a mesh axis runs over, the one named last changes fastest.
Arguments:
- amplitudes: bfloat16 [1024, 8192], P('row', 'col'), may hold values from -6 to 6
- intermediate: bfloat16 [8192, 1024], P('row', 'col'), may hold values from -0.0625 to 0.0625
Outputs:
- residual: float32 [8, 4, 32, 1024], P(None, 'col', None, ('row', 'rep'))
All inputs are finite; a program needn't handle non-finite values.
Results may differ from a plain program's by a relative error of at most 0.0029.
Values may be sent and summed in bfloat16 or wider, within the bound.
A program may use at most 128 MiB of HBM per device.

v0:
```python
import functools

import jax
import jax.numpy as jnp
from jax import lax
from jax.experimental import pallas as pl
from jax.experimental.pallas import tpu as pltpu
from jax.sharding import PartitionSpec as P

MESH = pl.DeviceIdType.MESH


def general(amplitudes, intermediate):
    rows_axis = lax.axis_size("row")
    cols_axis = lax.axis_size("col")
    depth_axis = lax.axis_size("rep")
    layer_index = lax.axis_index("rep")
    owner_rows = rows_axis * depth_axis
    fold_count = owner_rows // cols_axis
    local_rows = amplitudes.shape[0]
    band_rows = local_rows // depth_axis
    local_cols = intermediate.shape[1]
    slice_width = local_cols // owner_rows
    own_rows = lax.dynamic_slice_in_dim(amplitudes, layer_index * band_rows, band_rows, 0)
    all_weights = lax.all_gather(intermediate, "row", axis=0, tiled=True)
    summed = jnp.dot(
        lax.all_gather(own_rows, "col", axis=1, tiled=True),
        all_weights,
        preferred_element_type=jnp.float32,
    )
    cycle = summed.astype(jnp.bfloat16)
    spread_block = cycle.reshape(band_rows, fold_count, cols_axis, slice_width)
    direct = lax.all_to_all(spread_block, "col", split_axis=2, concat_axis=1, tiled=True).reshape(
        band_rows, owner_rows, slice_width
    )
    stacked = cycle.reshape(cols_axis, slice_width, fold_count, cols_axis * slice_width)
    mirror = lax.all_to_all(
        lax.all_to_all(stacked, "col", split_axis=0, concat_axis=2, tiled=True),
        ("row", "rep"),
        split_axis=2,
        concat_axis=0,
        tiled=True,
    )
    mirror_part = mirror.reshape(owner_rows, slice_width, band_rows).astype(jnp.float32)
    direct_part = jnp.transpose(direct, (1, 2, 0)).astype(jnp.float32)
    return (mirror_part + direct_part).reshape(owner_rows, 1, slice_width, band_rows)


def kernel(
    sizes, a_hbm, w_hbm, o_ref,
    a_v, w_v, relay, abuf, wbuf, p0, p1, r0, r1, turn, cyc, spread, perm, drecv, mrecv,
    in_sem, s_rly, s_a, s_b, s_w1, s_w2, s_fw, s_r0, s_r1, s_m, s_d,
    q_rly, q_a, q_w1, q_w2, q_r0, q_r1, q_m, q_d,
):
    rows, cols, depth, chunks = sizes
    r, c, x = lax.axis_index("row"), lax.axis_index("col"), lax.axis_index("rep")
    y, u = c // 2, c % 2
    oy, ou, ox = 1 - y, 1 - u, 1 - x
    sub, kc = a_v.shape[1:]
    width = w_v.shape[1]
    half = kc // 2
    slab = half // chunks
    strip = o_ref.shape[2]
    lanes = o_ref.shape[3]
    groups = width // (cols * strip)
    f32 = jnp.float32

    def rowset(side):
        return pl.ds(pl.multiple_of((x * 2 + side) * sub, sub), sub)

    def khalf(v):
        return pl.ds(v * half, half)

    def side_rows(side):
        return pl.ds(pl.multiple_of(side * half, half), half)

    loads = (
        pltpu.make_async_copy(a_hbm.at[rowset(oy)], a_v.at[0], in_sem.at[0]),
        pltpu.make_async_copy(a_hbm.at[rowset(y)], a_v.at[1], in_sem.at[1]),
        pltpu.make_async_copy(w_hbm.at[side_rows(x)], w_v.at[side_rows(x)], in_sem.at[2]),
        pltpu.make_async_copy(w_hbm.at[side_rows(ox)], w_v.at[side_rows(ox)], in_sem.at[3]),
    )
    for load in loads:
        load.start()

    barrier = pltpu.get_barrier_semaphore()
    total = rows * cols * depth
    me = (r * cols + c) * depth + x

    def greet(step, carry):
        other = (me + step) % total
        pl.semaphore_signal(
            barrier,
            inc=1,
            device_id=(other // (cols * depth), (other // depth) % cols, other % depth),
            device_id_type=MESH,
        )
        return carry

    lax.fori_loop(1, total, greet, 0)

    pl.semaphore_wait(barrier, total - 1)
    loads[0].wait()

    def remote(source, target, send, recv, to):
        return pltpu.make_async_remote_copy(
            src_ref=source, dst_ref=target, send_sem=send, recv_sem=recv,
            device_id=to, device_id_type=MESH,
        )

    def arrived(target, recv):
        pltpu.make_async_copy(target, target, recv).wait()

    pending = []

    def send(source, target, ssem, rsem, to, same=None):
        copy = remote(source, target, ssem, rsem, to)
        if same is None:
            copy.start()
            pending.append((copy, None))
            return

        @pl.when(same)
        def _():
            pltpu.make_async_copy(source, target, rsem).start()

        @pl.when(jnp.logical_not(same))
        def _():
            copy.start()

        pending.append((copy, jnp.logical_not(same)))

    rises = [(v, t) for v in range(2) for t in range(4)]

    def piece(v, t):
        return pl.ds(t * (sub // 4), sub // 4), khalf(v)

    for v, t in rises:
        at, ks = piece(v, t)
        send(
            a_v.at[0, at, ks], relay.at[at, ks], s_rly.at[v, t], q_rly.at[v, t],
            (r, oy * 2 + u, x),
        )
    loads[1].wait()
    for v in range(2):
        send(
            a_v.at[1, :, khalf(v)], abuf.at[r, :, khalf(v)], s_a.at[v], q_a.at[r, v],
            (c, y * 2 + v, x), jnp.logical_and(c == r, u == v),
        )
    loads[2].wait()

    def krows(side, n):
        return pl.ds(pl.multiple_of(side * half + n * slab, slab), slab)

    def wpart(ref, side, n, h):
        return ref.at[krows(side, n), pl.ds(h * lanes, lanes)]

    for h in range(depth):
        for n in range(chunks):
            send(
                wpart(w_v, x, n, h), wpart(wbuf, x, n, h), s_w1.at[h, n], q_w1.at[h, n],
                (r, oy * 2 + u, x),
            )

    far = oy * 2 + u
    for v, t in rises:
        at, ks = piece(v, t)
        arrived(relay.at[at, ks], q_rly.at[v, t])
        send(
            relay.at[at, ks], abuf.at[r, at, ks], s_b.at[v, t], q_a.at[r, v],
            (far, y * 2 + v, x), jnp.logical_and(far == r, u == v),
        )
    loads[3].wait()

    src = lax.broadcasted_iota(jnp.int32, (2 * width, 2 * width), 0)
    dst = lax.broadcasted_iota(jnp.int32, (2 * width, 2 * width), 1)
    lane_in = dst % strip
    grp = (dst // strip) % groups
    blk = (dst // (strip * groups)) % 2
    own = dst // (2 * strip * groups)
    perm[...] = jnp.where(
        src == blk * width + grp * (cols * strip) + own * strip + lane_in, 1.0, 0.0
    ).astype(jnp.bfloat16)

    order = (r, r + 1 - 2 * (r % 2), (r + rows // 2) % rows, rows - 1 - r)

    def forward_w(h, n):
        arrived(wpart(wbuf, x, n, h), q_w1.at[h, n])
        send(
            wpart(wbuf, x, n, h), wpart(wbuf, x, n, h), s_w2.at[h, n], q_w2.at[h, n], (r, c, ox)
        )

    def forward_a(i):
        mine = side_rows(u)
        arrived(abuf.at[i, :, mine], q_a.at[i, u])
        send(abuf.at[i, :, mine], abuf.at[i, :, mine], s_fw.at[i], q_a.at[i, u], (r, y * 2 + ou, x))

    def product(d):
        i = order[d]
        arrived(abuf.at[i, :, side_rows(ou)], q_a.at[i, ou])
        p0[i] = jnp.dot(abuf[i], w_v[...], preferred_element_type=f32)
        if d > 0:
            send(p0.at[i], r0.at[r], s_r0.at[i], q_r0.at[r], (i, c, x))

    hops = [(h, n) for h in range(depth) for n in range(chunks)]
    each = len(hops) // rows
    for d in range(rows):
        forward_a(order[d])
        product(d)
        for h, n in hops[d * each:(d + 1) * each]:
            forward_w(h, n)

    def add_product(side, n, h, first):
        part = jnp.dot(
            abuf[:, :, krows(side, n)].reshape(rows * sub, slab),
            wbuf[krows(side, n), pl.ds(h * lanes, lanes)],
            preferred_element_type=f32,
        ).reshape(rows, sub, lanes)
        p1[h] = part if first else p1[h] + part

    def other_product(h):
        for n in range(chunks):
            add_product(x, n, h, n == 0)
        for n in range(chunks):
            arrived(wpart(wbuf, ox, n, h), q_w2.at[h, n])
            add_product(ox, n, h, False)
        for d in range(1, rows):
            i = order[d]
            send(p1.at[h, i], r1.at[h, r], s_r1.at[h, i], q_r1.at[h, r], (i, c, x))

    def mirror(q, block, px):
        owner = block * 2 + u
        for pu in range(2):
            same = jnp.logical_and(jnp.logical_and(owner == r, px == x), pu == u)
            send(
                cyc.at[block, pl.ds(pu * strip, strip), pl.ds(px * lanes, lanes)],
                mrecv.at[r * depth + x],
                s_m.at[q, px, pu], q_m.at[r * depth + x], (owner, y * 2 + pu, px), same,
            )

    def finish_own():
        value = p0[r]
        for d in range(1, rows):
            i = order[d]
            arrived(r0.at[i], q_r0.at[i])
            value = value + r0[i]
        value = value.astype(jnp.bfloat16)
        cyc[y] = value
        for px in range(depth):
            mirror(0, y, px)
        rows_of = pl.ds(pl.multiple_of(y * width, width), width)
        turn[...] = jnp.dot(value, perm[rows_of, :], preferred_element_type=f32)

    def finish_other(h):
        value = p1[h, r]
        for d in range(1, rows):
            i = order[d]
            arrived(r1.at[h, i], q_r1.at[h, i])
            value = value + r1[h, i]
        value = value.astype(jnp.bfloat16)
        cyc[oy, :, pl.ds(h * lanes, lanes)] = value
        mirror(1, oy, h)
        rows_of = pl.ds(pl.multiple_of(oy * width + h * lanes, lanes), lanes)
        return turn[...] + jnp.dot(value, perm[rows_of, :], preferred_element_type=f32)

    other_product(0)
    finish_own()
    for h in range(1, depth):
        other_product(h)
        turn[...] = finish_other(h - 1)
    turned = finish_other(depth - 1)

    for to in range(cols):
        spread[to] = turned[:, to * lanes:(to + 1) * lanes].astype(jnp.bfloat16)
    place = pl.ds(pl.multiple_of(y * sub, sub), sub)
    for to in range(cols):
        send(spread.at[to], drecv.at[u, place, :], s_d.at[to], q_d.at[u, y], (r, to, x), c == to)

    for i in range(rows * depth):
        arrived(mrecv.at[i], q_m.at[i])
    for pu in range(2):
        for py in range(2):
            arrived(drecv.at[pu, pl.ds(py * sub, sub), :], q_d.at[pu, py])
        flipped = jnp.transpose(drecv[pu].astype(f32))
        for py in range(2):
            for g in range(groups):
                at = (py * groups + g) * strip
                a = (py * 2 + pu) * groups + g
                o_ref[a, 0] = mrecv[a].astype(f32) + flipped[at:at + strip, :]

    for copy, sent in pending:
        if sent is None:
            copy.wait_send()
        else:
            pl.when(sent)(copy.wait_send)


def planned(sizes, amplitudes, intermediate):
    rows, cols, depth, chunks = sizes
    band, kc = amplitudes.shape
    width = intermediate.shape[1]
    sub = band // (2 * depth)
    owners = rows * depth
    strip = width // owners
    lanes = band // depth
    bf16, f32 = jnp.bfloat16, jnp.float32
    dma = pltpu.SemaphoreType.DMA
    return pl.pallas_call(
        functools.partial(kernel, sizes),
        out_shape=jax.ShapeDtypeStruct((owners, 1, strip, lanes), f32),
        in_specs=[pl.BlockSpec(memory_space=pl.ANY)] * 2,
        out_specs=pl.BlockSpec(memory_space=pltpu.VMEM),
        scratch_shapes=[
            pltpu.VMEM((2, sub, kc), bf16),
            pltpu.VMEM((kc, width), bf16),
            pltpu.VMEM((sub, kc), bf16),
            pltpu.VMEM((rows, sub, kc), bf16),
            pltpu.VMEM((kc, width), bf16),
            pltpu.VMEM((rows, sub, width), f32),
            pltpu.VMEM((depth, rows, sub, lanes), f32),
            pltpu.VMEM((rows, sub, width), f32),
            pltpu.VMEM((depth, rows, sub, lanes), f32),
            pltpu.VMEM((sub, 2 * width), f32),
            pltpu.VMEM((2, sub, width), bf16),
            pltpu.VMEM((cols, sub, lanes), bf16),
            pltpu.VMEM((2 * width, 2 * width), bf16),
            pltpu.VMEM((2, 2 * sub, lanes), bf16),
            pltpu.VMEM((owners, strip, lanes), bf16),
            dma((4,)), dma((2, 4)), dma((2,)), dma((2, 4)), dma((depth, chunks)), dma((depth, chunks)),
            dma((rows,)), dma((rows,)), dma((depth, rows)), dma((2, depth, 2)), dma((cols,)),
            dma((2, 4)), dma((rows, 2)), dma((depth, chunks)), dma((depth, chunks)),
            dma((rows,)), dma((depth, rows)), dma((owners,)), dma((2, 2)),
        ],
        compiler_params=pltpu.CompilerParams(collective_id=0, has_side_effects=True),
    )(amplitudes, intermediate)


def solution(mesh):
    rows, cols, depth = (mesh.shape[name] for name in ("row", "col", "rep"))

    def local(amplitudes, intermediate):
        square = rows == cols == 2 * depth and depth == 2
        fits = amplitudes.shape[0] == intermediate.shape[1]
        if square and fits:
            return planned((rows, cols, depth, 4), amplitudes, intermediate)
        return general(amplitudes, intermediate)

    in_specs = (P("row", "col"), P("row", "col"))
    out_specs = P(None, "col", None, ("row", "rep"))
    return jax.shard_map(local, mesh=mesh, in_specs=in_specs, out_specs=out_specs, check_vma=False)
```

profile of v0, /device:TPU:5, one launch (start us, length us, event | category | flops | bytes accessed | tf_op | source)
XLA Modules:
  0.0 41.7 jit_solution(4270340389657369035)
XLA Ops:
  0.0 40.1 %shard_map.28 = f32[8,1,32,128]{3,2,1,0:T(8,128)} custom-call(bf16[256,2048]{1,0:T(8,128)(2,1)} %a_hbm.1, bf16[2048,256]{1,0:T(8,128)(2,1)} %w_hbm.1), custom_call_target="tpu_custom_call" | custom-call | tf_op jit(solution)/shard_map/pallas_call | solution.py:308
  40.1 1.6 %copy.4 = f32[8,1,32,128]{3,2,1,0:T(8,128)} copy(f32[8,1,32,128]{3,2,1,0:T(8,128)} %shard_map.28) | data formatting | bytes 262144
where the time goes:
time: 42.2 us; the launch traced here: 41.7 us
  Pallas kernels  40.1 us (95%)
  local copies, waits for them, and re-layouts  1.57 us (4%)
    pallas_call x1, Pallas kernels, planned(): pl.pallas_call(functools.partial(kernel, sizes), out_shape=jax.ShapeDtype...  40.1 us
    unnamed x1, local copies, waits for them, and re-layouts  1.57 us

commit v1 on v0

v1 whole, which is shorter than its diff:
```python
import functools

import jax
import jax.numpy as jnp
from jax import lax
from jax.experimental import pallas as pl
from jax.experimental.pallas import tpu as pltpu
from jax.sharding import PartitionSpec as P

MESH = pl.DeviceIdType.MESH


def general(amplitudes, intermediate):
    rows_axis = lax.axis_size("row")
    cols_axis = lax.axis_size("col")
    depth_axis = lax.axis_size("rep")
    layer_index = lax.axis_index("rep")
    owner_rows = rows_axis * depth_axis
    fold_count = owner_rows // cols_axis
    local_rows = amplitudes.shape[0]
    band_rows = local_rows // depth_axis
    local_cols = intermediate.shape[1]
    slice_width = local_cols // owner_rows
    own_rows = lax.dynamic_slice_in_dim(amplitudes, layer_index * band_rows, band_rows, 0)
    all_weights = lax.all_gather(intermediate, "row", axis=0, tiled=True)
    summed = jnp.dot(
        lax.all_gather(own_rows, "col", axis=1, tiled=True),
        all_weights,
        preferred_element_type=jnp.float32,
    )
    cycle = summed.astype(jnp.bfloat16)
    spread_block = cycle.reshape(band_rows, fold_count, cols_axis, slice_width)
    direct = lax.all_to_all(spread_block, "col", split_axis=2, concat_axis=1, tiled=True).reshape(
        band_rows, owner_rows, slice_width
    )
    stacked = cycle.reshape(cols_axis, slice_width, fold_count, cols_axis * slice_width)
    mirror = lax.all_to_all(
        lax.all_to_all(stacked, "col", split_axis=0, concat_axis=2, tiled=True),
        ("row", "rep"),
        split_axis=2,
        concat_axis=0,
        tiled=True,
    )
    mirror_part = mirror.reshape(owner_rows, slice_width, band_rows).astype(jnp.float32)
    direct_part = jnp.transpose(direct, (1, 2, 0)).astype(jnp.float32)
    return (mirror_part + direct_part).reshape(owner_rows, 1, slice_width, band_rows)


def kernel(
    sizes, a_hbm, w_hbm, o_ref,
    a_v, w_v, relay, abuf, part, rbuf, cyc, turn, mrecv, drecv,
    in_sem, s_all, q_rly, q_z, q_y, q_c, q_r, q_m, q_d, near_sem, far_sem, side_sem,
):
    rows, cols, depth, n = sizes
    r, c, x = lax.axis_index("row"), lax.axis_index("col"), lax.axis_index("rep")
    y, u = c // 2, c % 2
    oy, ou, ox = 1 - y, 1 - u, 1 - x
    band, kc = a_v.shape
    line = band // 2
    ch = line // n
    half = kc // 2
    strip = o_ref.shape[2]
    lanes = o_ref.shape[3]
    f32 = jnp.float32

    def khalf(v):
        return pl.ds(v * half, half)

    def mine(v):
        return pl.ds(pl.multiple_of(v * half, half), half)

    def line_rows(side):
        return pl.ds(pl.multiple_of(side * line, line), line)

    def hbm_rows(side):
        return pl.ds(pl.multiple_of(x * band + side * line, line), line)

    loads = (
        pltpu.make_async_copy(a_hbm.at[hbm_rows(oy)], a_v.at[line_rows(oy)], in_sem.at[0]),
        pltpu.make_async_copy(a_hbm.at[hbm_rows(y)], a_v.at[line_rows(y)], in_sem.at[1]),
        pltpu.make_async_copy(w_hbm, w_v, in_sem.at[2]),
    )
    for load in loads:
        load.start()

    barrier = pltpu.get_barrier_semaphore()
    core_mate, y_mate, x_mate = (r, y * 2 + ou, x), (r, oy * 2 + u, x), (r, c, ox)
    has_low, has_high = r > 0, r < rows - 1

    def signal(sem, to):
        pl.semaphore_signal(sem, inc=1, device_id=to, device_id_type=MESH)

    for to in (y_mate, core_mate, (r, oy * 2 + ou, x), x_mate):
        signal(barrier, to)

    @pl.when(has_low)
    def _():
        for v in range(2):
            signal(barrier, (r - 1, y * 2 + v, x))

    @pl.when(has_high)
    def _():
        for v in range(2):
            signal(barrier, (r + 1, y * 2 + v, x))

    inner = jnp.logical_and(has_low, has_high)
    pl.semaphore_wait(barrier, jnp.where(inner, 8, 6))

    pending = []
    count = [0]

    def send(source, target, rsem, to, same=None, local=None, only=None):
        index = count[0]
        count[0] += 1
        copy = pltpu.make_async_remote_copy(
            src_ref=source, dst_ref=target, send_sem=s_all.at[index], recv_sem=rsem,
            device_id=to, device_id_type=MESH,
        )
        if same is None:
            copy.start()
            pending.append((copy, None))
            return

        @pl.when(same)
        def _():
            pltpu.make_async_copy(source if local is None else local, target, rsem).start()

        @pl.when(jnp.logical_not(same))
        def _():
            copy.start()

        pending.append((copy, jnp.logical_not(same)))

    def arrived(target, recv):
        pltpu.make_async_copy(target, target, recv).wait()

    loads[0].wait()
    for i in range(n):
        at = pl.ds(pl.multiple_of(oy * line + i * ch, ch), ch)
        send(a_v.at[at], relay.at[i], q_rly.at[i], y_mate)

    signal(side_sem, x_mate)

    @pl.when(inner)
    def _():
        signal(near_sem, (r - 1, c, x))
        signal(near_sem, (r + 1, c, x))

    pl.semaphore_wait(near_sem, 1)

    @pl.when(r == 1)
    def _():
        signal(far_sem, (r - 1, c, x))

    @pl.when(r == rows - 2)
    def _():
        signal(far_sem, (r + 1, c, x))

    pl.when(jnp.logical_not(inner))(lambda: pl.semaphore_wait(far_sem, 1))

    loads[1].wait()

    def piece(i):
        return y * n + i

    for i in range(n):
        at = pl.ds(pl.multiple_of(y * line + i * ch, ch), ch)
        for v in range(2):
            send(
                a_v.at[at, khalf(v)], abuf.at[piece(i), r, :, khalf(v)], q_z.at[i, r],
                (c, y * 2 + v, x), jnp.logical_and(c == r, u == v),
            )

    far = oy * 2 + u
    order = (r, r + 1 - 2 * (r % 2), (r + rows // 2) % rows, rows - 1 - r)

    def relay_on(i):
        arrived(relay.at[i], q_rly.at[i])
        for v in range(2):
            send(
                relay.at[i, :, khalf(v)], abuf.at[piece(i), r, :, khalf(v)], q_z.at[i, r],
                (far, y * 2 + v, x), jnp.logical_and(far == r, u == v),
            )

    def to_core(j):
        ref = abuf.at[j, :, :, mine(u)]
        send(ref, ref, q_c.at[j], core_mate)

    def from_z(i):
        j = piece(i)
        for s in order:
            ref = abuf.at[j, s, :, mine(u)]
            arrived(ref, q_z.at[i, s])
            send(ref, ref, q_y.at[i, s], y_mate)
        to_core(j)

    def from_y(i):
        j = oy * n + i
        for s in order:
            arrived(abuf.at[j, s, :, mine(u)], q_y.at[i, s])
        to_core(j)

    def product(j):
        arrived(abuf.at[j, :, :, mine(ou)], q_c.at[j])
        value = jnp.dot(
            abuf[j].reshape(rows * ch, kc), w_v[...], preferred_element_type=f32
        )
        part[j] = value.reshape(rows, ch, value.shape[1])
        for s in order[1:]:
            send(part.at[j, s], rbuf.at[j, r], q_r.at[j, r], (s, c, x))

    def total(j):
        value = part[j, r]
        for s in order[1:]:
            arrived(rbuf.at[j, s], q_r.at[j, s])
            value = value + rbuf[j, s]
        cyc[pl.ds(pl.multiple_of(j * ch, ch), ch), :] = value.astype(jnp.bfloat16)

    per = strip // ch

    def finish(side, g):
        m = side * (cols // 2) + g
        for i in range(per):
            total(side * n + g * per + i)
        for px in range(depth):
            send(
                cyc.at[pl.ds(pl.multiple_of(m * strip, strip), strip), pl.ds(px * lanes, lanes)],
                mrecv.at[r * depth + x], q_m.at[r * depth + x], (c, m, px),
                jnp.logical_and(jnp.logical_and(c == r, m == c), px == x),
            )

    relay_on(0)
    relay_on(1)
    relay_on(2)
    from_z(0)
    relay_on(3)
    loads[2].wait()
    pl.semaphore_wait(side_sem, 1)
    from_z(1)
    product(y * n)
    from_y(0)
    from_z(2)
    product(y * n + 1)
    product(oy * n)
    from_y(1)
    from_z(3)
    product(y * n + 2)
    product(oy * n + 1)
    from_y(2)
    product(y * n + 3)
    product(oy * n + 2)
    from_y(3)
    product(oy * n + 3)
    finish(y, 0)
    finish(oy, 0)
    finish(y, 1)
    finish(oy, 1)

    turn[...] = jnp.transpose(cyc[...].astype(f32)).astype(jnp.bfloat16)
    for to in range(cols):
        for b in range(2):
            at = c * 2 + b
            send(
                turn.at[pl.ds(b * lanes + to * strip, strip)], drecv.at[at], q_d.at[at], (r, to, x), c == to,
            )

    for i in range(rows * depth):
        arrived(mrecv.at[i], q_m.at[i])
        arrived(drecv.at[i], q_d.at[i])
        o_ref[i, 0] = mrecv[i].astype(f32) + drecv[i].astype(f32)

    for copy, sent in pending:
        if sent is None:
            copy.wait_send()
        else:
            pl.when(sent)(copy.wait_send)


def planned(sizes, amplitudes, intermediate):
    rows, cols, depth, n = sizes
    kc, width = intermediate.shape
    band = amplitudes.shape[0] // depth
    owners = rows * depth
    strip = width // owners
    ch = band // (2 * n)
    bf16, f32 = jnp.bfloat16, jnp.float32
    dma, plain = pltpu.SemaphoreType.DMA, pltpu.SemaphoreType.REGULAR
    return pl.pallas_call(
        functools.partial(kernel, sizes),
        out_shape=jax.ShapeDtypeStruct((owners, 1, strip, band), f32),
        in_specs=[pl.BlockSpec(memory_space=pl.ANY)] * 2,
        out_specs=pl.BlockSpec(memory_space=pltpu.VMEM),
        scratch_shapes=[
            pltpu.VMEM((band, kc), bf16),
            pltpu.VMEM((kc, width), bf16),
            pltpu.VMEM((n, ch, kc), bf16),
            pltpu.VMEM((2 * n, rows, ch, kc), bf16),
            pltpu.VMEM((2 * n, rows, ch, width), f32),
            pltpu.VMEM((2 * n, rows, ch, width), f32),
            pltpu.VMEM((band, width), bf16),
            pltpu.VMEM((width, band), bf16),
            pltpu.VMEM((owners, strip, band), bf16),
            pltpu.VMEM((owners, strip, band), bf16),
            dma((3,)), dma((128,)), dma((n,)), dma((n, rows)), dma((n, rows)), dma((2 * n,)),
            dma((2 * n, rows)), dma((owners,)), dma((owners,)), plain, plain, plain,
        ],
        compiler_params=pltpu.CompilerParams(collective_id=0, has_side_effects=True),
    )(amplitudes, intermediate)


def solution(mesh):
    rows, cols, depth = (mesh.shape[name] for name in ("row", "col", "rep"))

    def local(amplitudes, intermediate):
        square = rows == cols == 2 * depth and depth == 2
        band, width = amplitudes.shape[0] // depth, intermediate.shape[1]
        fits = amplitudes.shape[0] == width and band % 128 == 0 and amplitudes.shape[1] == intermediate.shape[0]
        if square and fits and band == 128:
            return planned((rows, cols, depth, 4), amplitudes, intermediate)
        return general(amplitudes, intermediate)

    in_specs = (P("row", "col"), P("row", "col"))
    out_specs = P(None, "col", None, ("row", "rep"))
    return jax.shard_map(local, mesh=mesh, in_specs=in_specs, out_specs=out_specs, check_vma=False)
```

time: 42.2 us -> 42.1 us (level); the launches traced: 41.7 us -> 42 us
  no operation moved by 1% of the time
where the time goes in v1:
time: 42.1 us; the launch traced here: 42 us
  Pallas kernels  40.4 us (96%)
  local copies, waits for them, and re-layouts  1.57 us (4%)
    pallas_call x1, Pallas kernels, planned(): pl.pallas_call(functools.partial(kernel, sizes), out_shape=jax.ShapeDtype...  40.4 us
    unnamed x1, local copies, waits for them, and re-layouts  1.57 us

profile of v1, /device:TPU:5, one launch (start us, length us, event | category | flops | bytes accessed | tf_op | source)
XLA Modules:
  0.0 42.0 jit_solution(18318925224972050299)
XLA Ops:
  0.0 40.4 %shard_map.28 = f32[8,1,32,128]{3,2,1,0:T(8,128)} custom-call(bf16[256,2048]{1,0:T(8,128)(2,1)} %a_hbm.1, bf16[2048,256]{1,0:T(8,128)(2,1)} %w_hbm.1), custom_call_target="tpu_custom_call" | custom-call | tf_op jit(solution)/shard_map/pallas_call | solution.py:288
  40.4 1.6 %copy.4 = f32[8,1,32,128]{3,2,1,0:T(8,128)} copy(f32[8,1,32,128]{3,2,1,0:T(8,128)} %shard_map.28) | data formatting | bytes 262144

commit v2 on v1

v2 whole, which is shorter than its diff:
```python
import functools

import jax
import jax.numpy as jnp
from jax import lax
from jax.experimental import pallas as pl
from jax.experimental.pallas import tpu as pltpu
from jax.sharding import PartitionSpec as P

MESH = pl.DeviceIdType.MESH


def general(amplitudes, intermediate):
    rows_axis = lax.axis_size("row")
    cols_axis = lax.axis_size("col")
    depth_axis = lax.axis_size("rep")
    layer_index = lax.axis_index("rep")
    owner_rows = rows_axis * depth_axis
    fold_count = owner_rows // cols_axis
    local_rows = amplitudes.shape[0]
    band_rows = local_rows // depth_axis
    local_cols = intermediate.shape[1]
    slice_width = local_cols // owner_rows
    own_rows = lax.dynamic_slice_in_dim(amplitudes, layer_index * band_rows, band_rows, 0)
    all_weights = lax.all_gather(intermediate, "row", axis=0, tiled=True)
    summed = jnp.dot(
        lax.all_gather(own_rows, "col", axis=1, tiled=True),
        all_weights,
        preferred_element_type=jnp.float32,
    )
    cycle = summed.astype(jnp.bfloat16)
    spread_block = cycle.reshape(band_rows, fold_count, cols_axis, slice_width)
    direct = lax.all_to_all(spread_block, "col", split_axis=2, concat_axis=1, tiled=True).reshape(
        band_rows, owner_rows, slice_width
    )
    stacked = cycle.reshape(cols_axis, slice_width, fold_count, cols_axis * slice_width)
    mirror = lax.all_to_all(
        lax.all_to_all(stacked, "col", split_axis=0, concat_axis=2, tiled=True),
        ("row", "rep"),
        split_axis=2,
        concat_axis=0,
        tiled=True,
    )
    mirror_part = mirror.reshape(owner_rows, slice_width, band_rows).astype(jnp.float32)
    direct_part = jnp.transpose(direct, (1, 2, 0)).astype(jnp.float32)
    return (mirror_part + direct_part).reshape(owner_rows, 1, slice_width, band_rows)


RELAY, OWN, RELAYED, KEPT, ACROSS, NEAR, AWAY, PARTIAL, OUTWARD, PASSED, MIRROR, DIRECT, LAST = range(13)


def kernel(
    sizes, a_hbm, w_hbm, o_ref,
    a_v, w_v, relay, abuf, part, acc, rbuf, cyc, turn, mrecv, drecv,
    in_sem, s_all, q_rly, q_z, q_y, q_near, q_away, q_acc, q_r0, q_r1, q_r2, q_out, near_sem, far_sem, side_sem,
):
    rows, cols, depth, n = sizes
    r, c, x = lax.axis_index("row"), lax.axis_index("col"), lax.axis_index("rep")
    y, u = c // 2, c % 2
    oy, ou, ox = 1 - y, 1 - u, 1 - x
    band, kc = a_v.shape
    line = band // 2
    ch = line // n
    half = kc // 2
    strip = o_ref.shape[2]
    lanes = o_ref.shape[3]
    per = n // 2
    f32 = jnp.float32

    def khalf(v):
        return pl.ds(v * half, half)

    def mine(v):
        return pl.ds(pl.multiple_of(v * half, half), half)

    def line_rows(side):
        return pl.ds(pl.multiple_of(side * line, line), line)

    def chunk_rows(side, i):
        return pl.ds(pl.multiple_of(side * line + i * ch, ch), ch)

    def hbm_rows(side):
        return pl.ds(pl.multiple_of(x * band + side * line, line), line)

    loads = (
        pltpu.make_async_copy(a_hbm.at[hbm_rows(oy)], a_v.at[line_rows(oy)], in_sem.at[0]),
        pltpu.make_async_copy(a_hbm.at[hbm_rows(y)], a_v.at[line_rows(y)], in_sem.at[1]),
        pltpu.make_async_copy(w_hbm, w_v, in_sem.at[2]),
    )
    for load in loads:
        load.start()

    barrier = pltpu.get_barrier_semaphore()
    core_mate, y_mate, x_mate = (r, y * 2 + ou, x), (r, oy * 2 + u, x), (r, c, ox)
    has_low, has_high = r > 0, r < rows - 1

    def signal(sem, to):
        pl.semaphore_signal(sem, inc=1, device_id=to, device_id_type=MESH)

    for to in (y_mate, core_mate, (r, oy * 2 + ou, x), x_mate):
        signal(barrier, to)

    @pl.when(has_low)
    def _():
        for v in range(2):
            signal(barrier, (r - 1, y * 2 + v, x))

    @pl.when(has_high)
    def _():
        for v in range(2):
            signal(barrier, (r + 1, y * 2 + v, x))

    inner = jnp.logical_and(has_low, has_high)
    outer = jnp.logical_not(inner)
    pl.semaphore_wait(barrier, jnp.where(inner, 8, 6))

    mate, near, away = r + 1 - 2 * (r % 2), 2 * (r // 2), 2 - 2 * (r // 2)
    home = y == r // 2
    over = oy * 2 + u

    def remote(source, target, group, rsem, to):
        return pltpu.make_async_remote_copy(
            src_ref=source, dst_ref=target, send_sem=s_all.at[group], recv_sem=rsem,
            device_id=to, device_id_type=MESH,
        )

    def send(source, target, group, rsem, to, same=None):
        copy = remote(source, target, group, rsem, to)
        if same is None:
            copy.start()
        else:
            pl.when(same)(lambda: pltpu.make_async_copy(source, target, rsem).start())
            pl.when(jnp.logical_not(same))(copy.start)

    def arrived(target, recv):
        pltpu.make_async_copy(target, target, recv).wait()

    loads[0].wait()
    for i in range(n):
        send(a_v.at[chunk_rows(oy, i)], relay.at[i], RELAY, q_rly.at[i], y_mate)

    signal(side_sem, x_mate)

    @pl.when(inner)
    def _():
        signal(near_sem, (r - 1, c, x))
        signal(near_sem, (r + 1, c, x))

    reach = jnp.abs(c - r)
    pl.when(reach > 1)(lambda: pl.semaphore_wait(near_sem, 1))
    pl.when(reach > 2)(lambda: pl.semaphore_wait(far_sem, 1))
    loads[1].wait()

    def slot(i, plane):
        return jnp.where(plane == r, i // per, jnp.where(plane == mate, 2 + i // per, 4 + i))

    def along(source, i, plane, group):
        for v in range(2):
            send(
                source(khalf(v)), abuf.at[y * n + i, r, :, khalf(v)], group, q_z.at[slot(i, plane)],
                (plane, y * 2 + v, x), jnp.logical_and(plane == r, u == v),
            )

    def own(i):
        along(lambda ks: a_v.at[chunk_rows(y, i), ks], i, c, OWN)

    own(0)
    own(1)
    pl.when(reach <= 1)(lambda: pl.semaphore_wait(near_sem, 1))
    pl.when(r == 1)(lambda: signal(far_sem, (r - 1, c, x)))
    pl.when(r == rows - 2)(lambda: signal(far_sem, (r + 1, c, x)))
    pl.when(jnp.logical_and(outer, reach <= 2))(lambda: pl.semaphore_wait(far_sem, 1))

    def relay_on(i):
        arrived(relay.at[i], q_rly.at[i])
        along(lambda ks: relay.at[i, :, ks], i, over, RELAYED)

    def keep(i):
        for v in range(2):
            source, target = a_v.at[chunk_rows(oy, i), khalf(v)], abuf.at[oy * n + i, r, :, khalf(v)]
            recv = q_y.at[i // per]
            copy = remote(source, target, KEPT, recv, core_mate)
            here = jnp.logical_and(c == r, u == v)
            pl.when(here)(lambda: pltpu.make_async_copy(source, target, recv).start())
            pl.when(jnp.logical_and(c == r, u != v))(copy.start)

    def own_block(side, g):
        return abuf.at[pl.ds(side * n + g * per, per), r, :, mine(u)]

    def mate_block(side, g):
        return abuf.at[pl.ds(side * n + g * per, per), mate, :, mine(u)]

    def away_block(j, v):
        return abuf.at[j, pl.ds(away, 2), :, mine(v)]

    def own_z(g):
        ref = own_block(y, g)
        arrived(ref, q_z.at[g])
        copy = remote(ref, ref, ACROSS, q_y.at[g], y_mate)
        pl.when(home)(copy.start)

    def mate_z(g):
        ref = mate_block(y, g)
        arrived(ref, q_z.at[2 + g])
        send(ref, ref, ACROSS, q_y.at[2 + g], y_mate)

    def near_to_core(side, g):
        ref = abuf.at[pl.ds(side * n + g * per, per), pl.ds(near, 2), :, mine(u)]
        send(ref, ref, NEAR, q_near.at[side * 2 + g], core_mate)

    def away_to_core(j):
        send(away_block(j, u), away_block(j, u), AWAY, q_away.at[j], core_mate)

    def away_z(i):
        ref = away_block(y * n + i, u)
        arrived(ref, q_z.at[4 + i])
        send(ref, ref, ACROSS, q_y.at[4 + i], y_mate)
        away_to_core(y * n + i)

    def near_y(g):
        arrived(own_block(oy, g), q_y.at[g])
        arrived(mate_block(oy, g), q_y.at[2 + g])
        near_to_core(oy, g)

    def away_y(i):
        arrived(away_block(oy * n + i, u), q_y.at[4 + i])
        away_to_core(oy * n + i)

    def near_product(side, g):
        chunks, pair = pl.ds(side * n + g * per, per), pl.ds(near, 2)
        arrived(abuf.at[chunks, pair, :, mine(ou)], q_near.at[side * 2 + g])
        value = jnp.dot(
            abuf[chunks, pair].reshape(2 * per * ch, kc), w_v[...], preferred_element_type=f32
        )
        part[chunks, pair] = value.reshape(per, 2, ch, value.shape[1])
        send(part.at[chunks, mate], rbuf.at[chunks, 0], PARTIAL, q_r0.at[side * 2 + g], (mate, c, x))

    def product(side, i):
        j = side * n + i
        pair = pl.ds(away, 2)
        arrived(away_block(j, ou), q_away.at[j])
        value = jnp.dot(
            abuf[j, pair].reshape(2 * ch, kc), w_v[...], preferred_element_type=f32
        )
        part[j, pair] = value.reshape(2, ch, value.shape[1])
        if i < n - 1:
            outward = remote(part.at[j, pair], acc.at[side * (n - 1) + i], OUTWARD, q_acc.at[side * (n - 1) + i], (mate, c, x))
            pl.when(outer)(outward.start)
            return
        for f in range(2):
            send(part.at[j, away + f], rbuf.at[j, 1 + r % 2], LAST, q_r2.at[side], (away + f, c, x))

    def pass_on(side, i):
        j, m = side * n + i, side * 2 + i // per
        copies = [
            remote(part.at[j, away + f], rbuf.at[j, 1], PASSED, q_r1.at[m], (away + f, c, x)) for f in range(2)
        ]

        @pl.when(inner)
        def _():
            arrived(acc.at[side * (n - 1) + i], q_acc.at[side * (n - 1) + i])
            for f in range(2):
                part[j, away + f] = part[j, away + f] + acc[side * (n - 1) + i, f]
                copies[f].start()

    def finish(side, g):
        m = side * 2 + g
        chunks = pl.ds(side * n + g * per, per)
        arrived(rbuf.at[chunks, 0], q_r0.at[m])
        through = per - g
        arrived(rbuf.at[pl.ds(side * n + g * per, through), 1], q_r1.at[m])
        early = pl.ds(side * n + g * per, through)
        value = part[early, r] + rbuf[early, 0] + rbuf[early, 1]
        if g:
            j = side * n + n - 1
            arrived(rbuf.at[j, pl.ds(1, 2)], q_r2.at[side])
            ends = part[j, r] + rbuf[j, 0] + rbuf[j, 1] + rbuf[j, 2]
            value = jnp.concatenate([value, ends[None]], axis=0)
        at = pl.ds(pl.multiple_of(m * strip, strip), strip)
        cyc[at, :] = value.reshape(strip, value.shape[2]).astype(jnp.bfloat16)
        for px in range(depth):
            send(
                cyc.at[at, pl.ds(px * lanes, lanes)], mrecv.at[r * depth + x], MIRROR, q_out.at[0], (c, m, px),
                jnp.logical_and(jnp.logical_and(c == r, m == c), px == x),
            )

    def flush(group, ref):
        pltpu.make_async_copy(ref, ref, s_all.at[group]).wait()

    relay_on(0)
    own(2)
    relay_on(1)
    own(3)
    for i in range(n):
        keep(i)
    own_z(0)
    relay_on(2)
    relay_on(3)
    own_z(1)
    mate_z(0)
    near_to_core(y, 0)
    away_z(0)
    mate_z(1)
    near_to_core(y, 1)
    loads[2].wait()
    near_product(y, 0)
    product(y, 0)
    away_z(1)
    away_y(0)
    near_product(y, 1)
    near_y(0)
    product(y, 1)
    away_z(2)
    pl.semaphore_wait(side_sem, 1)
    product(oy, 0)
    pass_on(y, 0)
    away_y(1)
    near_product(oy, 0)
    pass_on(y, 1)
    away_z(3)
    product(y, 2)
    near_y(1)
    product(oy, 1)
    pass_on(oy, 0)
    away_y(2)
    near_product(oy, 1)
    product(y, 3)
    pass_on(y, 2)
    pass_on(oy, 1)
    away_y(3)
    product(oy, 2)
    finish(y, 0)
    product(oy, 3)
    pass_on(oy, 2)
    finish(oy, 0)
    finish(y, 1)
    finish(oy, 1)

    turn[...] = jnp.transpose(cyc[...].astype(f32)).astype(jnp.bfloat16)
    for to in range(cols):
        for b in range(2):
            at = c * 2 + b
            send(
                turn.at[pl.ds(b * lanes + to * strip, strip)], drecv.at[at], DIRECT, q_out.at[1], (r, to, x), c == to,
            )

    flush(RELAY, relay)
    for group, plane in ((OWN, c), (RELAYED, over)):
        pl.when(plane == r)(lambda: flush(group, relay.at[:, :, khalf(0)]))
        pl.when(plane != r)(lambda: flush(group, relay))
    pl.when(c == r)(lambda: flush(KEPT, relay.at[:, :, khalf(0)]))
    pl.when(home)(lambda: flush(ACROSS, abuf.at[pl.ds(0, n), :, :, khalf(0)]))
    pl.when(jnp.logical_not(home))(lambda: flush(ACROSS, abuf.at[pl.ds(0, n), pl.ds(0, rows - 1), :, khalf(0)]))
    flush(NEAR, abuf.at[:, pl.ds(0, 2), :, khalf(0)])
    flush(AWAY, abuf.at[:, pl.ds(0, 2), :, khalf(0)])
    flush(PARTIAL, part.at[:, 0])
    pl.when(outer)(lambda: flush(OUTWARD, acc))
    pl.when(inner)(lambda: flush(PASSED, acc))
    flush(LAST, rbuf.at[pl.ds(0, 2), pl.ds(1, 2)])

    arrived(mrecv, q_out.at[0])
    arrived(drecv, q_out.at[1])
    for i in range(rows * depth):
        o_ref[i, 0] = mrecv[i].astype(f32) + drecv[i].astype(f32)

    pl.when(c == r)(lambda: flush(MIRROR, mrecv.at[pl.ds(0, rows * depth - 1)]))
    pl.when(c != r)(lambda: flush(MIRROR, mrecv))
    flush(DIRECT, drecv.at[pl.ds(0, rows * depth - 2)])


def planned(sizes, amplitudes, intermediate):
    rows, cols, depth, n = sizes
    kc, width = intermediate.shape
    band = amplitudes.shape[0] // depth
    owners = rows * depth
    strip = width // owners
    ch = band // (2 * n)
    bf16, f32 = jnp.bfloat16, jnp.float32
    dma, plain = pltpu.SemaphoreType.DMA, pltpu.SemaphoreType.REGULAR
    return pl.pallas_call(
        functools.partial(kernel, sizes),
        out_shape=jax.ShapeDtypeStruct((owners, 1, strip, band), f32),
        in_specs=[pl.BlockSpec(memory_space=pl.ANY)] * 2,
        out_specs=pl.BlockSpec(memory_space=pltpu.VMEM),
        scratch_shapes=[
            pltpu.VMEM((band, kc), bf16),
            pltpu.VMEM((kc, width), bf16),
            pltpu.VMEM((n, ch, kc), bf16),
            pltpu.VMEM((2 * n, rows, ch, kc), bf16),
            pltpu.VMEM((2 * n, rows, ch, width), f32),
            pltpu.VMEM((2 * (n - 1), 2, ch, width), f32),
            pltpu.VMEM((2 * n, 3, ch, width), f32),
            pltpu.VMEM((band, width), bf16),
            pltpu.VMEM((width, band), bf16),
            pltpu.VMEM((owners, strip, band), bf16),
            pltpu.VMEM((owners, strip, band), bf16),
            dma((3,)), dma((13,)), dma((n,)), dma((4 + n,)), dma((4 + n,)), dma((4,)), dma((2 * n,)), dma((2 * n,)),
            dma((4,)), dma((4,)), dma((2,)), dma((2,)), plain, plain, plain,
        ],
        compiler_params=pltpu.CompilerParams(
            collective_id=0, has_side_effects=True, vmem_limit_bytes=56_000_000
        ),
    )(amplitudes, intermediate)


def solution(mesh):
    rows, cols, depth = (mesh.shape[name] for name in ("row", "col", "rep"))

    def local(amplitudes, intermediate):
        square = rows == cols == 2 * depth and depth == 2
        band, width = amplitudes.shape[0] // depth, intermediate.shape[1]
        fits = amplitudes.shape[0] == width and band % 128 == 0 and amplitudes.shape[1] == intermediate.shape[0]
        if square and fits and band == 128:
            return planned((rows, cols, depth, 4), amplitudes, intermediate)
        return general(amplitudes, intermediate)

    in_specs = (P("row", "col"), P("row", "col"))
    out_specs = P(None, "col", None, ("row", "rep"))
    return jax.shard_map(local, mesh=mesh, in_specs=in_specs, out_specs=out_specs, check_vma=False)
```

time: 42.1 us -> 36.7 us (0.87)
  Pallas kernels: 40.4 us -> 35.9 us
  local copies, waits for them, and re-layouts: 1.57 us -> 0.66 us
    pallas_call x1, Pallas kernels: 40.4 us -> 35.9 us  [planned(): pl.pallas_call(functools.partial(kernel, sizes), out_shape=jax.ShapeDtype...]
    unnamed x1, local copies, waits for them, and re-layouts: 1.57 us -> 0.66 us
where the time goes in v2:
time: 36.7 us; the launch traced here: 36.6 us
  Pallas kernels  35.9 us (98%)
  local copies, waits for them, and re-layouts  0.66 us (2%)
    pallas_call x1, Pallas kernels, planned(): pl.pallas_call(functools.partial(kernel, sizes), out_shape=jax.ShapeDtype...  35.9 us

profile of v2, /device:TPU:5, one launch (start us, length us, event | category | flops | bytes accessed | tf_op | source)
XLA Modules:
  0.0 36.6 jit_solution(13585288754539424088)
XLA Ops:
  0.0 35.9 %shard_map.28 = f32[8,1,32,128]{3,2,1,0:T(8,128)S(1)} custom-call(bf16[256,2048]{1,0:T(8,128)(2,1)} %a_hbm.1, bf16[2048,256]{1,0:T(8,128)(2,1)} %w_hbm.1), custom_call_target="tpu_custom_call" | custom-call | tf_op jit(solution)/shard_map/pallas_call | solution.py:380
  35.9 0.7 %copy.4 = f32[8,1,32,128]{3,2,1,0:T(8,128)} copy(f32[8,1,32,128]{3,2,1,0:T(8,128)S(1)} %shard_map.28) | data formatting | bytes 262144
